TPU v7x, 32 devices: a whole 2x2x4 slice. The times are simulated.
32 devices in a mesh: blk: 16 (over z, x, core), tp: 2 (over y).
Axes of the slice: x: 2, y: 2, z: 4, core: 2. Of those that a mesh axis runs over, the one named last changes fastest.
Arguments:
- weights: float32 [16, 1024, 1024], P('blk', None, 'tp'), may hold values from -6 to 6
- copies: bfloat16 [16, 1024, 1024], P('blk', None, 'tp'), may hold values from -60 to 60
- copies_mixed: bfloat16 [16, 1024, 1024], P('blk', None, 'tp'), may hold values from -64 to 64
- tracker: bfloat16 [16, 1024, 1024], P('blk', None, 'tp'), may hold values from -6 to 6
- tracker_copy: bfloat16 [16, 1024, 1024], P('blk', None, 'tp'), may hold values from -6 to 6
- tracker_mixed: bfloat16 [16, 1024, 1024], P('blk', None, 'tp'), may hold values from -6 to 6
- grad_prev: bfloat16 [16, 1024, 1024], P('blk', None, 'tp'), may hold values from -3 to 3
- tokens: bfloat16 [16, 1024, 1024], P('blk', 'tp'), may hold values from -12 to 12
- image_ids: int32 [16, 1024], P('blk'), may hold values from 0 to 5, never falling along the last dimension, each value on 1 to 197 neighbouring positions
- key_weight: bfloat16 [1024, 1024], P(None, 'tp'), may hold values from -0.1875 to 0.1875
- value_weight: bfloat16 [1024, 1024], P(None, 'tp'), may hold values from -0.1875 to 0.1875
- out_grad: bfloat16 [16, 1024, 1024], P('blk', None, 'tp'), may hold values from -48 to 48
- row_picks: int32 [16, 2, 64], replicated, may hold values from 0 to 1023, as said below
Outputs:
- weights_new: float32 [16, 1024, 1024], P('blk', None, 'tp')
- copies_new: bfloat16 [16, 1024, 1024], P('blk', None, 'tp')
- mixed_new: bfloat16 [16, 1024, 1024], P('blk', None, 'tp')
- tracker_new: bfloat16 [16, 1024, 1024], P('blk', None, 'tp')
- tracker_copy_new: bfloat16 [16, 1024, 1024], P('blk', None, 'tp')
- tracker_mixed_new: bfloat16 [16, 1024, 1024], P('blk', None, 'tp')
- grad_new: bfloat16 [16, 1024, 1024], P('blk', None, 'tp')
- consensus: float32 [], replicated
Inputs may be any that keep to these rules, and one draw needn't show every extreme that they name: `image_ids`: never falling along a replica's tokens; an image holds 1 to 197 tokens. `row_picks`: each row lists 64 different rows; the same picks serve every head shard of a replica.
All inputs are finite; a program needn't handle non-finite values.
Results may differ from a plain program's by a relative error of at most 0.0095.
The roundings to bfloat16 on the way count: a program that leaves them out, or rounds other values in their place, can miss the bound.
Values may be sent and summed in bfloat16 or wider, within the bound.
A program may use at most 128 MiB of HBM per device.

v0:
```python
import functools

import jax
import jax.numpy as jnp
from jax import lax
from jax.experimental import pallas as pl
from jax.experimental.pallas import tpu as pltpu
from jax.sharding import PartitionSpec as P

HD = 64
SEG_MOST = 197
TILE = 128

mixing_rate = 0.2
step_rate = 0.5

ANY = pl.BlockSpec(memory_space=pl.ANY)
VMEM = pl.BlockSpec(memory_space=pltpu.VMEM)
HBM = pl.BlockSpec(memory_space=pltpu.HBM)


def contract(left, right, left_dim, right_dim):
    return lax.dot_general(
        left, right, (((left_dim,), (right_dim,)), ((), ())), preferred_element_type=jnp.float32
    )


def one_hot(picks, total_rows):
    columns = lax.broadcasted_iota(jnp.int32, (picks.shape[0], total_rows), 1)
    return (picks[:, None] == columns).astype(jnp.bfloat16)


def picked_rows(picks, total_rows):
    rows = lax.broadcasted_iota(jnp.int32, (total_rows, picks.shape[0]), 0)
    return jnp.any(rows == picks[None, :], axis=1, keepdims=True)


def replica_picks(row_picks, offset):
    count = lax.axis_size("blk")
    rank = lax.rem(lax.axis_index("blk") + offset + count, count)
    return lax.dynamic_index_in_dim(row_picks, rank, 0, keepdims=False)


def mix_stream(pieces, row_picks, stream, total_rows):
    picks = jnp.concatenate([replica_picks(row_picks, o)[stream] for o in (-1, 0, 1)], axis=0)
    values = jnp.concatenate(pieces, axis=0)
    return contract(one_hot(picks, total_rows), values, 0, 0) / 3.0


def gossip_kernel(
    blk_count, tp_count, values, part, lower, upper, total, slots, send_sem, recv_sem, part_sems
):
    blk, tp = lax.axis_index("blk"), lax.axis_index("tp")
    count = blk_count * tp_count
    me = blk * tp_count + tp
    mesh_type = pl.DeviceIdType.MESH
    barrier = pltpu.get_barrier_semaphore()

    def device(distance):
        flat = lax.rem(me + distance, count)
        return (flat // tp_count, lax.rem(flat, tp_count))

    def greet(distance, carry):
        pl.semaphore_signal(barrier, inc=1, device_id=device(distance), device_id_type=mesh_type)
        return carry

    lax.fori_loop(1, count, greet, 0)
    pl.semaphore_wait(barrier, count - 1)
    after = lax.rem(blk + 1, blk_count)
    before = lax.rem(blk + blk_count - 1, blk_count)
    up = pltpu.make_async_remote_copy(
        values, lower, send_sem.at[0], recv_sem.at[0], device_id=(after, tp), device_id_type=mesh_type
    )
    down = pltpu.make_async_remote_copy(
        values, upper, send_sem.at[1], recv_sem.at[1], device_id=(before, tp), device_id_type=mesh_type
    )
    up.start()
    down.start()

    def send(distance, carry):
        pltpu.make_async_remote_copy(
            part,
            slots.at[distance - 1],
            part_sems.at[0],
            part_sems.at[1],
            device_id=device(distance),
            device_id_type=mesh_type,
        ).start()
        return carry

    lax.fori_loop(1, count, send, 0)
    pltpu.make_async_copy(slots, slots, part_sems.at[1]).wait()
    pltpu.make_async_copy(slots, slots, part_sems.at[0]).wait()
    total[...] = jnp.sum(slots[...], axis=0) + part[...]
    up.wait()
    down.wait()


def gossip(values, part):
    blk_count, tp_count = lax.axis_size("blk"), lax.axis_size("tp")
    same = jax.ShapeDtypeStruct(values.shape, values.dtype)
    return pl.pallas_call(
        functools.partial(gossip_kernel, blk_count, tp_count),
        out_shape=(same, same, jax.ShapeDtypeStruct(part.shape, part.dtype)),
        in_specs=[VMEM, VMEM],
        out_specs=(VMEM, VMEM, VMEM),
        scratch_shapes=[
            pltpu.VMEM((blk_count * tp_count - 1,) + part.shape, part.dtype),
            pltpu.SemaphoreType.DMA((2,)),
            pltpu.SemaphoreType.DMA((2,)),
            pltpu.SemaphoreType.DMA((2,)),
        ],
        compiler_params=pltpu.CompilerParams(collective_id=0, has_side_effects=True),
        cost_estimate=pl.CostEstimate(flops=10000, bytes_accessed=10000000, transcendentals=0),
    )(values, part)


def attend(lows, total_rows, qs, ks, vs, og, qg, ids_col, ids_row, bias):
    width = qs.shape[1]
    pair = 2 * HD
    lane = lax.broadcasted_iota(jnp.int32, (1, pair), 1)
    first = jnp.where(lane < HD, 1.0, 0.0).astype(jnp.bfloat16)
    second = jnp.where(lane < HD, 0.0, 1.0).astype(jnp.bfloat16)
    reach = SEG_MOST - 1
    for low in lows:
        start = max(0, (low - reach) // TILE * TILE)
        end = min(total_rows, -(-(low + TILE + reach) // TILE) * TILE)
        span = end - start
        same = ids_col[low : low + TILE, :] == ids_row[:, start:end]
        tile_bias = jnp.where(same, 0.0, -1e30)
        bias[:TILE, :span] = tile_bias
        bias[TILE:, :span] = tile_bias

        @pl.loop(0, width // pair, unroll=2 if width // pair % 2 == 0 else 1)
        def _(index):
            columns = pl.ds(pl.multiple_of(index * pair, pair), pair)
            query = qs[low : low + TILE, columns]
            outer = og[low : low + TILE, columns]
            keyed = ks[start:end, columns]
            valued = vs[start:end, columns]
            queries = jnp.concatenate([query * first, query * second], axis=0)
            outers = jnp.concatenate([outer * first, outer * second], axis=0)
            scores = contract(queries, keyed, 1, 1) + bias[:, :span]
            out_proj = contract(outers, valued, 1, 1)
            exponent = jnp.exp(scores - jnp.max(scores, axis=-1, keepdims=True))
            inverse = 1.0 / jnp.sum(exponent, axis=-1, keepdims=True)
            centre = jnp.sum(exponent * out_proj, axis=-1, keepdims=True) * inverse
            score_grad = (exponent * ((out_proj - centre) * (inverse * HD ** (-0.5)))).astype(
                jnp.bfloat16
            )
            both = jnp.dot(score_grad, keyed, preferred_element_type=jnp.float32)
            qg[low : low + TILE, columns] = jnp.where(lane < HD, both[:TILE], both[TILE:]).astype(
                jnp.bfloat16
            )


def project(start, steps, tok, qw, kw, vw, qs, ks, vs, proj):
    @pl.loop(0, steps)
    def _(step):
        rows = pl.ds(pl.multiple_of(start + step * proj, proj), proj)
        block = tok[rows, :]
        query = jnp.dot(block, qw[...], preferred_element_type=jnp.float32).astype(jnp.bfloat16)
        qs[rows, :] = (query.astype(jnp.float32) * HD ** (-0.5)).astype(jnp.bfloat16)
        ks[rows, :] = jnp.dot(block, kw[...], preferred_element_type=jnp.float32).astype(jnp.bfloat16)
        vs[rows, :] = jnp.dot(block, vw[...], preferred_element_type=jnp.float32).astype(jnp.bfloat16)


def piece_rows(index, rank, local, count):
    start = lax.rem(rank - index + count, count) * local
    return pl.ds(pl.multiple_of(start, local), local)


def span_limit(total_rows):
    return min(total_rows, TILE + 2 * (-(-(SEG_MOST - 1) // TILE) * TILE))


def gradient_kernel(count, *refs):
    pieces = refs[:count]
    (query_w, key_w, value_w, out_grad, ids_col, ids_row, picks_row, picks_col) = refs[count : count + 8]
    fields = refs[count + 8 : count + 12]
    grad_out, tracker_out, copy_out, kept = refs[count + 12 : count + 16]
    scratch = refs[count + 16 :]
    tok, qw, kw, vw, og, tr, tm, tc, gp, qs, ks, vs, qg, upd, bias, go, to, co, tok_sems, sems, out_sems = scratch
    total_rows, model_width = tok.shape
    rank = lax.axis_index("tp")

    loads = []
    for shift in range(count):
        where = piece_rows(shift, rank, pieces[0].shape[0], count)
        loads.append(pltpu.make_async_copy(pieces[shift], tok.at[where], tok_sems.at[shift]))
    sources = (query_w, key_w, value_w, out_grad) + fields
    for index, (source, target) in enumerate(zip(sources, (qw, kw, vw, og, tr, tm, tc, gp))):
        loads.append(pltpu.make_async_copy(source, target, sems.at[index]))
    for load in loads:
        load.start()
    for load in loads[: count + 4]:
        load.wait()

    project(0, total_rows // 256, tok, qw, kw, vw, qs, ks, vs, 256)
    attend(range(0, total_rows, TILE), total_rows, qs, ks, vs, og, qg, ids_col, ids_row, bias)

    for load in loads[count + 4 :]:
        load.wait()

    @pl.loop(0, model_width // TILE)
    def _(step):
        base = pl.multiple_of(step * TILE, TILE)
        rows = pl.ds(base, TILE)
        product = contract(tok[:, rows], qg[...], 0, 0)
        grad = (product * model_width ** (-0.5)).astype(jnp.bfloat16)
        copy = tc[rows, :].astype(jnp.float32)
        new = (
            tr[rows, :].astype(jnp.float32)
            + mixing_rate * (tm[rows, :].astype(jnp.float32) - copy)
            + grad.astype(jnp.float32)
            - gp[rows, :].astype(jnp.float32)
        ).astype(jnp.bfloat16)
        change = new.astype(jnp.float32) - copy
        index = lax.broadcasted_iota(jnp.int32, (TILE, picks_row.shape[1]), 0) + base
        hits = jnp.where(index == picks_row[...], 1.0, 0.0)
        picked = jnp.max(hits, axis=1, keepdims=True)
        go[rows, :] = grad
        to[rows, :] = new
        co[rows, :] = (copy + change * picked).astype(jnp.bfloat16)
        upd[rows, :] = change.astype(jnp.bfloat16)
        for slot, (source, target) in enumerate(((go, grad_out), (to, tracker_out), (co, copy_out))):
            pltpu.make_async_copy(source.at[rows], target.at[rows], out_sems.at[slot]).start()

    columns = lax.broadcasted_iota(jnp.int32, (picks_col.shape[0], model_width), 1)
    matrix = jnp.where(picks_col[...] == columns, 1.0, 0.0).astype(jnp.bfloat16)
    kept[...] = jnp.dot(matrix, upd[...], preferred_element_type=jnp.float32).astype(jnp.bfloat16)
    for slot, (source, target) in enumerate(((go, grad_out), (to, tracker_out), (co, copy_out))):
        pltpu.make_async_copy(source, target, out_sems.at[slot]).wait()


def gradient_stage(pieces, query_weight, key_weight, value_weight, out_grad, image_row, picks, fields):
    count = len(pieces)
    model_width = pieces[0].shape[1]
    total_rows = out_grad.shape[0]
    width = query_weight.shape[1]
    bf16 = jnp.bfloat16
    field = jax.ShapeDtypeStruct((model_width, width), bf16)
    weight = pltpu.VMEM((model_width, width), bf16)
    row_block = pltpu.VMEM((total_rows, width), bf16)
    return pl.pallas_call(
        functools.partial(gradient_kernel, count),
        out_shape=(field, field, field, jax.ShapeDtypeStruct((picks.shape[0], width), bf16)),
        in_specs=[ANY] * (count + 4) + [VMEM] * 4 + [ANY] * 4,
        out_specs=(ANY, ANY, ANY, VMEM),
        scratch_shapes=[pltpu.VMEM((total_rows, model_width), bf16)]
        + [weight] * 3
        + [row_block]
        + [weight] * 4
        + [row_block] * 4
        + [weight, pltpu.VMEM((2 * TILE, span_limit(total_rows)), jnp.float32)]
        + [weight] * 3
        + [
            pltpu.SemaphoreType.DMA((count,)),
            pltpu.SemaphoreType.DMA((8,)),
            pltpu.SemaphoreType.DMA((3,)),
        ],
        compiler_params=pltpu.CompilerParams(vmem_limit_bytes=56 * 2**20),
        cost_estimate=pl.CostEstimate(
            flops=8 * total_rows * model_width * width + 6 * total_rows * 640 * width,
            bytes_accessed=24 * model_width * width,
            transcendentals=total_rows * 640 * width // HD,
        ),
    )(
        *pieces,
        query_weight,
        key_weight,
        value_weight,
        out_grad,
        image_row.reshape(total_rows, 1),
        image_row.reshape(1, total_rows),
        picks.reshape(1, -1),
        picks.reshape(-1, 1),
        *fields,
    )


IMAGES = 6
PACK = 16
QUERY_ROWS = 224
KEY_ROWS = 256
MESH = pl.DeviceIdType.MESH


def token_chunks(local):
    edges = [0]
    for count in range(3, IMAGES):
        need = -(-(count * SEG_MOST - local) // 16) * 16
        edges.append(min(local, max(need, edges[-1])))
    edges.append(local)
    return list(zip(edges[:-1], edges[1:]))


def pick_column(picks, blk, stream):
    row = picks[blk, stream : stream + 1, :].astype(jnp.float32)
    size = row.shape[1]
    rows = lax.broadcasted_iota(jnp.int32, (size, size), 0)
    columns = lax.broadcasted_iota(jnp.int32, (size, size), 1)
    return jnp.sum(jnp.where(rows == columns, row, 0.0), axis=1, keepdims=True)


def hot_rows(column, total_rows):
    index = lax.broadcasted_iota(jnp.int32, (column.shape[0], total_rows), 1)
    return jnp.where(column == index.astype(jnp.float32), 1.0, 0.0).astype(jnp.bfloat16)


def picked_mask(picks, blk, stream, base, rows):
    row = picks[blk, stream : stream + 1, :]
    index = lax.broadcasted_iota(jnp.int32, (rows, row.shape[1]), 0) + base
    return jnp.max(jnp.where(index == row, 1.0, 0.0), axis=1, keepdims=True)


def window_start(low, ref, rows):
    return jnp.minimum(low // PACK, ref.shape[0] - rows // PACK)


def window(ref, block, rows, columns):
    parts = [ref[block + index, :, columns] for index in range(rows // PACK)]
    return jnp.concatenate(parts, axis=0)


def attend_image(slot, low, high, qs, ks, vs, og, qg):
    width = qs.shape[2]
    pair = 2 * HD
    lane = lax.broadcasted_iota(jnp.int32, (1, pair), 1)
    first = jnp.where(lane < HD, 1.0, 0.0).astype(jnp.bfloat16)
    second = jnp.where(lane < HD, 0.0, 1.0).astype(jnp.bfloat16)
    query_block = window_start(low, qs, QUERY_ROWS)
    key_block = window_start(low, qs, KEY_ROWS)
    position = lax.broadcasted_iota(jnp.int32, (1, KEY_ROWS), 1) + key_block * PACK
    bias = jnp.where((position >= low) & (position < high), 0.0, -1e30)
    row = lax.broadcasted_iota(jnp.int32, (QUERY_ROWS, pair), 0) + query_block * PACK
    inside = (row >= low) & (row < high)

    @pl.loop(0, width // pair, unroll=2)
    def _(index):
        columns = pl.ds(pl.multiple_of(index * pair, pair), pair)
        query = window(qs, query_block, QUERY_ROWS, columns)
        outer = window(og, query_block, QUERY_ROWS, columns)
        keyed = window(ks, key_block, KEY_ROWS, columns)
        valued = window(vs, key_block, KEY_ROWS, columns)
        queries = jnp.concatenate([query * first, query * second], axis=0)
        outers = jnp.concatenate([outer * first, outer * second], axis=0)
        scores = contract(queries, keyed, 1, 1) + bias
        out_proj = contract(outers, valued, 1, 1)
        exponent = jnp.exp(scores - jnp.max(scores, axis=-1, keepdims=True))
        inverse = 1.0 / jnp.sum(exponent, axis=-1, keepdims=True)
        centre = jnp.sum(exponent * out_proj, axis=-1, keepdims=True) * inverse
        score_grad = (exponent * ((out_proj - centre) * (inverse * HD ** (-0.5)))).astype(
            jnp.bfloat16
        )
        both = jnp.dot(score_grad, keyed, preferred_element_type=jnp.float32)
        merged = jnp.where(lane < HD, both[:QUERY_ROWS], both[QUERY_ROWS:])
        qg[slot, :, columns] = jnp.where(inside, merged, 0.0).astype(jnp.bfloat16)


def step_kernel(blk_count, chunks, *refs):
    (weights, copies, mixed, tracker, tracker_copy, tracker_mixed, grad_prev) = refs[:7]
    (tokens, ids, key_weight, value_weight, out_grad, row_picks) = refs[7:13]
    (w_out, copy_out, mix_out, grad_out, new_out, held_out, tm, values, spread, total) = refs[13:23]
    (wt, cp, mx, tr, tc, gp, kw, vw, og, qw, upd, tok, recv) = refs[23:36]
    (qs, ks, vs, qg, acc, base, id_row, picks, heard, hot, part, slots, group, other) = refs[36:50]
    (load_sem, send_tok, recv_tok, near, rise, fall, send_row, recv_row, sum_sem) = refs[50:]

    blk, tp = lax.axis_index("blk"), lax.axis_index("tp")
    planes = blk_count // 4
    plane = blk // 4
    blocks = tokens.shape[0]
    width = qs.shape[2]
    model_width = tok.shape[2]
    kept = row_picks.shape[2]
    partner = (blk, 1 - tp)
    after = (lax.rem(blk + 1, blk_count), tp)
    before = (lax.rem(blk + blk_count - 1, blk_count), tp)
    flip_two = (blk + 2 - 4 * (lax.rem(blk, 4) // 2), tp)
    flip_one = (blk + 1 - 2 * lax.rem(blk, 2), tp)
    below = (jnp.maximum(blk - 4, 0), tp)
    above = (jnp.minimum(blk + 4, blk_count - 1), tp)
    lowest = plane == 0
    highest = plane == planes - 1

    barrier = pltpu.get_barrier_semaphore()
    for device in (partner, flip_one, flip_two):
        pl.semaphore_signal(barrier, inc=1, device_id=device, device_id_type=MESH)

    def tell(lower, upper):
        @pl.when(jnp.logical_not(lowest))
        def _():
            pl.semaphore_signal(lower, inc=1, device_id=below, device_id_type=MESH)

        @pl.when(jnp.logical_not(highest))
        def _():
            pl.semaphore_signal(upper, inc=1, device_id=above, device_id_type=MESH)

    def hear(lower, upper):
        @pl.when(jnp.logical_not(highest))
        def _():
            pl.semaphore_wait(lower, 1)

        @pl.when(jnp.logical_not(lowest))
        def _():
            pl.semaphore_wait(upper, 1)

    tell(barrier, barrier)

    own = pl.ds(tp * blocks, blocks)
    far = pl.ds((1 - tp) * blocks, blocks)
    sources = (tokens, row_picks, ids, weights, copies, mixed, tracker)
    sources += (key_weight, value_weight, out_grad, tracker_copy, tracker_mixed, grad_prev)
    targets = (tok.at[own], picks, id_row, wt, cp, mx, tr, kw, vw, og, tc, tm, gp)
    loads = [
        pltpu.make_async_copy(source, target, load_sem.at[index])
        for index, (source, target) in enumerate(zip(sources, targets))
    ]
    for load in loads:
        load.start()
    loads[0].wait()
    pl.semaphore_wait(barrier, 5 - lowest.astype(jnp.int32) - highest.astype(jnp.int32))

    sends = []
    for index, (start, end) in enumerate(chunks):
        size = end - start
        first = blocks * tp + jnp.where(tp == 0, blocks - end, start)
        send = pltpu.make_async_remote_copy(
            tok.at[pl.ds(first, size)],
            recv.at[start:end],
            send_tok.at[index],
            recv_tok.at[index],
            device_id=partner,
            device_id_type=MESH,
        )
        send.start()
        sends.append(send)

    pl.semaphore_signal(near.at[0], inc=1, device_id=flip_two, device_id_type=MESH)

    for target in (qs, ks, vs, tok):
        target[far] = jnp.zeros((blocks,) + target.shape[1:], jnp.bfloat16)
    for load in loads[1:7]:
        load.wait()

    for stream, target in enumerate((hot, spread)):
        for index, shift in enumerate((blk_count - 1, 0, 1)):
            rank = lax.rem(blk + shift, blk_count)
            target[index * kept : (index + 1) * kept, :] = hot_rows(
                pick_column(picks, rank, stream), model_width
            )

    @pl.loop(0, model_width // TILE)
    def _(step):
        start = pl.multiple_of(step * TILE, TILE)
        rows = pl.ds(start, TILE)
        copy = cp[rows, :].astype(jnp.float32)
        new = (
            wt[rows, :]
            + mixing_rate * (mx[rows, :].astype(jnp.float32) - copy)
            - step_rate * tr[rows, :].astype(jnp.float32)
        )
        change = new - copy
        w_out[rows, :] = new
        query = (new * model_width ** (-0.5)).astype(jnp.bfloat16)
        qw[rows, :] = query * jnp.bfloat16(HD ** (-0.5))
        upd[rows, :] = change.astype(jnp.bfloat16)
        picked = picked_mask(picks, blk, 0, start, TILE)
        copy_out[rows, :] = jnp.where(picked > 0.5, copy + change, copy).astype(jnp.bfloat16)

    middle = slice(kept, 2 * kept)
    heard[middle, :] = jnp.dot(
        hot[middle, :], upd[...], preferred_element_type=jnp.float32
    ).astype(jnp.bfloat16)

    pl.semaphore_wait(near.at[0], 1)
    pl.semaphore_signal(near.at[1], inc=1, device_id=flip_one, device_id_type=MESH)

    edge = []
    for image in range(IMAGES + 1):
        edge.append(jnp.sum(jnp.where(id_row[...] < image, 1, 0)))

    def bounds(slot):
        low = jnp.where(tp == 0, edge[slot], edge[IMAGES - 1 - slot])
        high = jnp.where(tp == 0, edge[slot + 1], edge[IMAGES - slot])
        return low, high

    def project_block(block, rows):
        flat = block.reshape(-1, model_width)
        for target, weight in ((qs, qw), (ks, kw), (vs, vw)):
            result = jnp.dot(flat, weight[...], preferred_element_type=jnp.float32)
            target[rows] = result.astype(jnp.bfloat16).reshape(-1, PACK, width)

    loads[7].wait()
    loads[8].wait()

    @pl.loop(0, 2)
    def _(step):
        rows = pl.ds(tp * blocks + step * (blocks // 2), blocks // 2)
        project_block(tok[rows], rows)

    pl.semaphore_wait(near.at[1], 1)
    for stage in range(planes - 2):
        tell(fall.at[stage], rise.at[stage])
        if stage == 0:
            loads[9].wait()
            attend_image(0, *bounds(0), qs, ks, vs, og, qg)
        if stage == 1:
            attend_image(1, *bounds(1), qs, ks, vs, og, qg)
        hear(fall.at[stage], rise.at[stage])
    if planes < 3:
        loads[9].wait()
    for slot in range(min(2, planes - 2), 2):
        attend_image(slot, *bounds(slot), qs, ks, vs, og, qg)

    def swap(source, target, index):
        moves = []
        for way, (device, slot) in enumerate(((after, 0), (before, 2))):
            move = pltpu.make_async_remote_copy(
                source.at[middle],
                target.at[slot * kept : (slot + 1) * kept],
                send_row.at[2 * index + way],
                recv_row.at[2 * index + way],
                device_id=device,
                device_id_type=MESH,
            )
            move.start()
            moves.append(move)
        return moves

    param = swap(heard, heard, 0)

    def take(index):
        start, end = chunks[index]
        size = end - start
        sends[index].wait_recv()
        first = blocks * (1 - tp) + jnp.where(tp == 0, start, blocks - end)
        rows = pl.ds(first, size)
        block = recv[start:end]
        tok[rows] = block
        project_block(block, rows)

    take(0)
    attend_image(2, *bounds(2), qs, ks, vs, og, qg)

    for move in param:
        move.wait()
    part[...] = jnp.zeros_like(part)

    @pl.loop(0, model_width // TILE)
    def _(step):
        rows = pl.ds(pl.multiple_of(step * TILE, TILE), TILE)
        gain = contract(hot[:, rows], heard[...], 0, 0) / 3.0
        new = (mx[rows, :].astype(jnp.float32) + gain).astype(jnp.bfloat16)
        mix_out[rows, :] = new
        gap = new.astype(jnp.float32) - copy_out[rows, :].astype(jnp.float32)
        square = gap * gap
        folded = sum(square[:, at : at + 128] for at in range(0, width, 128))
        part[...] += jnp.sum(folded.reshape(TILE // 8, 8, 128), axis=0)

    slots[pl.ds(blk, 1)] = part[...][None]

    def share(distance):
        return pltpu.make_async_remote_copy(
            part,
            slots.at[blk],
            sum_sem.at[0],
            sum_sem.at[1],
            device_id=(lax.rem(blk + distance, blk_count), tp),
            device_id_type=MESH,
        )

    @pl.loop(1, blk_count)
    def _(distance):
        share(distance).start()

    for load in loads[10:]:
        load.wait()

    @pl.loop(0, model_width // TILE)
    def _(step):
        rows = pl.ds(pl.multiple_of(step * TILE, TILE), TILE)
        copy = tc[rows, :].astype(jnp.float32)
        base[rows, :] = (
            tr[rows, :].astype(jnp.float32)
            + mixing_rate * (tm[rows, :].astype(jnp.float32) - copy)
            - gp[rows, :].astype(jnp.float32)
        )

    take(1)
    attend_image(3, *bounds(3), qs, ks, vs, og, qg)

    def product(slots_used, rows):
        result = 0.0
        for slot in slots_used:
            block = window_start(bounds(slot)[0], tok, QUERY_ROWS)
            result += contract(window(tok, block, QUERY_ROWS, rows), qg[slot], 0, 0)
        return result

    @pl.loop(0, model_width // TILE)
    def _(step):
        rows = pl.ds(pl.multiple_of(step * TILE, TILE), TILE)
        acc[rows, :] = product(range(4), rows)

    most = pl.ds(0, blk_count - 1)
    for way in range(2):
        pltpu.make_async_copy(slots.at[most], slots.at[most], sum_sem.at[way]).wait()
    group[...] = jnp.sum(slots[...], axis=0)
    cross = pltpu.make_async_remote_copy(
        group, other, sum_sem.at[2], sum_sem.at[3], device_id=partner, device_id_type=MESH
    )
    cross.start()

    take(2)
    attend_image(4, *bounds(4), qs, ks, vs, og, qg)
    take(3)
    attend_image(5, *bounds(5), qs, ks, vs, og, qg)

    @pl.loop(0, model_width // TILE)
    def _(step):
        start = pl.multiple_of(step * TILE, TILE)
        rows = pl.ds(start, TILE)
        gradient = acc[rows, :] + product((4, 5), rows)
        grad = (gradient * model_width ** (-0.5)).astype(jnp.bfloat16)
        copy = tc[rows, :].astype(jnp.float32)
        new = (base[rows, :] + grad.astype(jnp.float32)).astype(jnp.bfloat16)
        change = new.astype(jnp.float32) - copy
        picked = picked_mask(picks, blk, 1, start, TILE)
        grad_out[rows, :] = grad
        new_out[rows, :] = new
        held_out[rows, :] = jnp.where(picked > 0.5, copy + change, copy).astype(jnp.bfloat16)
        upd[rows, :] = change.astype(jnp.bfloat16)

    values[middle, :] = jnp.dot(
        spread[middle, :], upd[...], preferred_element_type=jnp.float32
    ).astype(jnp.bfloat16)
    track = swap(values, values, 1)

    cross.wait()
    total[...] = group[...] + other[...]
    for send in sends:
        send.wait_send()
    for move in track:
        move.wait()


def finish_kernel(entries, *refs):
    sources, tm, values, spread, total = refs[:6], refs[6], refs[7], refs[8], refs[9]
    targets, mix_target, sum_target = refs[10:16], refs[16], refs[17]
    mixed, sems = refs[18:]
    model_width = tm.shape[0]
    moves = [
        pltpu.make_async_copy(source, target, sems.at[index])
        for index, (source, target) in enumerate(zip(sources, targets))
    ]
    for move in moves:
        move.start()

    @pl.loop(0, model_width // (2 * TILE))
    def _(step):
        rows = pl.ds(pl.multiple_of(step * 2 * TILE, 2 * TILE), 2 * TILE)
        gain = contract(spread[:, rows], values[...], 0, 0) / 3.0
        mixed[rows, :] = (tm[rows, :].astype(jnp.float32) + gain).astype(jnp.bfloat16)
        pltpu.make_async_copy(mixed.at[rows], mix_target.at[rows], sems.at[6]).start()

    sum_target[...] = jnp.full((1, 1), 0.0, jnp.float32) + jnp.sum(total[...]) / entries
    for move in moves:
        move.wait()
    pltpu.make_async_copy(mixed, mix_target, sems.at[6]).wait()


def fused_step(blk_count, arrays):
    (weights, _, _, _, _, _, _) = arrays[:7]
    (tokens, ids, key_weight, value_weight, out_grad, row_picks) = arrays[7:]
    model_width, width = weights.shape
    packed_tokens = tokens.reshape(-1, PACK, model_width)
    packed_grad = out_grad.reshape(-1, PACK, width)
    arrays = arrays[:7] + (packed_tokens, ids, key_weight, value_weight, packed_grad, row_picks)
    local = tokens.shape[0]
    total_rows = ids.shape[1]
    kept = row_picks.shape[2]
    chunks = [(start // PACK, end // PACK) for start, end in token_chunks(local)]
    planes = blk_count // 4
    bf16, f32 = jnp.bfloat16, jnp.float32
    field = pltpu.VMEM((model_width, width), bf16)
    wide = pltpu.VMEM((model_width, width), f32)
    rows = pltpu.VMEM((total_rows // PACK, PACK, width), bf16)
    lanes = pltpu.VMEM((8, 128), f32)
    heard = pltpu.VMEM((3 * kept, width), bf16)
    hot = pltpu.VMEM((3 * kept, model_width), bf16)
    dma = pltpu.SemaphoreType.DMA
    held = pl.pallas_call(
        functools.partial(step_kernel, blk_count, chunks),
        out_shape=(wide,) + (field,) * 6 + (heard, hot, lanes),
        in_specs=[HBM] * 13,
        out_specs=(VMEM,) * 10,
        scratch_shapes=[wide]
        + [field] * 7
        + [rows, field, field]
        + [pltpu.VMEM((count // PACK, PACK, model_width), bf16) for count in (total_rows, local)]
        + [rows] * 3
        + [pltpu.VMEM((IMAGES, QUERY_ROWS, width), bf16), wide, wide]
        + [pltpu.VMEM(ids.shape, jnp.int32), pltpu.VMEM(row_picks.shape, jnp.int32), heard, hot]
        + [lanes, pltpu.VMEM((blk_count, 8, 128), f32), lanes, lanes]
        + [dma((13,)), dma((len(chunks),)), dma((len(chunks),))]
        + [pltpu.SemaphoreType.REGULAR((2,))]
        + [pltpu.SemaphoreType.REGULAR((max(planes - 2, 1),))] * 2
        + [dma((4,)), dma((4,)), dma((4,))],
        compiler_params=pltpu.CompilerParams(
            collective_id=0, has_side_effects=True, vmem_limit_bytes=44 * 2**20
        ),
        cost_estimate=pl.CostEstimate(
            flops=8 * total_rows * model_width * width,
            bytes_accessed=24 * model_width * width,
            transcendentals=total_rows * 256 * width // HD,
        ),
    )(*arrays)
    flat = jax.ShapeDtypeStruct((model_width, width), bf16)
    entries = float(blk_count * model_width * model_width)
    outs = pl.pallas_call(
        functools.partial(finish_kernel, entries),
        out_shape=(jax.ShapeDtypeStruct((model_width, width), f32),)
        + (flat,) * 6
        + (jax.ShapeDtypeStruct((1, 1), f32),),
        in_specs=[VMEM] * 10,
        out_specs=(HBM,) * 7 + (VMEM,),
        scratch_shapes=[field, dma((7,))],
        compiler_params=pltpu.CompilerParams(vmem_limit_bytes=8 * 2**20),
        cost_estimate=pl.CostEstimate(
            flops=model_width * width * 400,
            bytes_accessed=16 * model_width * width,
            transcendentals=0,
        ),
    )(*held)
    weights_new, copies_new, mixed_new, grad_new, tracker_new, held_new, mixed_back, total = outs
    return (
        weights_new[None],
        copies_new[None],
        mixed_new[None],
        tracker_new[None],
        held_new[None],
        mixed_back[None],
        grad_new[None],
        total[0, 0],
    )


def fits_fused(blk_count, local, model_width, width):
    enough = (IMAGES - 1) * SEG_MOST <= 2 * local and 2 * SEG_MOST <= local <= 3 * SEG_MOST
    shapes = local % 256 == 0 and model_width % 256 == 0 and width % (4 * HD) == 0
    return enough and shapes and blk_count % 4 == 0 and blk_count >= 8


def device_step(
    weights,
    copies,
    copies_mixed,
    tracker,
    tracker_copy,
    tracker_mixed,
    grad_prev,
    tokens,
    image_ids,
    key_weight,
    value_weight,
    out_grad,
    row_picks,
):
    model_width = weights.shape[1]
    blk_count, tp_count = lax.axis_size("blk"), lax.axis_size("tp")
    local = tokens.shape[1]
    if tp_count == 2 and fits_fused(blk_count, local, *weights.shape[1:]):
        fields = (weights, copies, copies_mixed, tracker, tracker_copy, tracker_mixed, grad_prev)
        return fused_step(
            blk_count,
            tuple(field[0] for field in fields)
            + (tokens[0], image_ids, key_weight, value_weight, out_grad[0], row_picks),
        )
    pieces = [tokens[0]]
    for shift in range(1, tp_count):
        hop = [(i, (i + shift) % tp_count) for i in range(tp_count)]
        pieces.append(lax.ppermute(tokens[0], "tp", hop))
    own_picks = replica_picks(row_picks, 0)
    copy_value = copies[0].astype(jnp.float32)
    mixed_value = copies_mixed[0].astype(jnp.float32)
    weights_new = (
        weights[0]
        + mixing_rate * (mixed_value - copy_value)
        - step_rate * tracker[0].astype(jnp.float32)
    )
    query_weight = (weights_new * model_width ** (-0.5)).astype(jnp.bfloat16)
    update = weights_new - copy_value
    picked = picked_rows(own_picks[0], model_width)
    copies_new = jnp.where(picked, copy_value + update, copy_value).astype(jnp.bfloat16)
    kept = contract(
        one_hot(own_picks[0], model_width), update.astype(jnp.bfloat16), 1, 0
    ).astype(jnp.bfloat16)
    up = [(i, (i + 1) % blk_count) for i in range(blk_count)]
    down = [(j, i) for i, j in up]
    lower = lax.ppermute(kept, "blk", up)
    upper = lax.ppermute(kept, "blk", down)
    mixed_new = (
        mixed_value + mix_stream([lower, kept, upper], row_picks, 0, model_width)
    ).astype(jnp.bfloat16)
    gap = mixed_new.astype(jnp.float32) - copies_new.astype(jnp.float32)
    part = jnp.broadcast_to(jnp.sum(gap * gap)[None, None], (8, 128))

    part, query_weight = lax.optimization_barrier((part, query_weight))
    grad_new, tracker_new, tracker_copy_new, kept = gradient_stage(
        pieces,
        query_weight,
        key_weight,
        value_weight,
        out_grad[0],
        image_ids[0],
        own_picks[1],
        (tracker[0], tracker_mixed[0], tracker_copy[0], grad_prev[0]),
    )
    lower, upper, total = gossip(kept, part)
    tracker_mixed_new = (
        tracker_mixed[0].astype(jnp.float32)
        + mix_stream([lower, kept, upper], row_picks, 1, model_width)
    ).astype(jnp.bfloat16)
    entries = float(blk_count * model_width * model_width)
    return (
        weights_new[None],
        copies_new[None],
        mixed_new[None],
        tracker_new[None],
        tracker_copy_new[None],
        tracker_mixed_new[None],
        grad_new[None],
        total[0, 0] / entries,
    )


def solution(mesh):
    field = P("blk", None, "tp")
    return jax.shard_map(
        device_step,
        mesh=mesh,
        in_specs=(field,) * 7
        + (P("blk", "tp", None), P("blk", None), P(None, "tp"), P(None, "tp"), field, P()),
        out_specs=(field,) * 7 + (P(),),
        check_vma=False,
    )
```

profile of v0, /device:TPU:0, one launch (start us, length us, event | category | flops | bytes accessed | tf_op | source)
XLA Modules:
  0.0 47.2 jit_solution(6299420089567065934)
XLA Ops:
  0.6 0.0 copy-start
  0.6 1.2 %copy-done = bf16[1,1024,512]{2,1,0:T(8,128)(2,1)S(1)} copy-done((bf16[1,1024,512]{2,1,0:T(8,128)(2,1)S(1)}, bf16[1,1024,512]{2,1,0:T(8,128)(2,1)}, u32[]{:S(2)}) %copy-start) | copy-done | bytes 1048600
  1.9 0.0 copy-start.1
  1.9 0.7 %copy-done.1 = s32[16,2,64]{2,1,0:T(2,128)S(1)} copy-done((s32[16,2,64]{2,1,0:T(2,128)S(1)}, s32[16,2,64]{2,1,0:T(2,128)}, u32[]{:S(2)}) %copy-start.1) | copy-done | bytes 8216
  2.6 0.0 copy-start.2
  2.6 0.7 %copy-done.2 = s32[1,1024]{1,0:T(1,128)S(1)} copy-done((s32[1,1024]{1,0:T(1,128)S(1)}, s32[1,1024]{1,0:T(1,128)}, u32[]{:S(2)}) %copy-start.2) | copy-done | bytes 4120
  3.3 40.0 %shard_map.188 = (f32[1024,512]{1,0:T(8,128)S(1)}, bf16[1024,512]{1,0:T(8,128)(2,1)S(1)}, bf16[1024,512]{1,0:T(8,128)(2,1)S(1)}, bf16[1024,512]{1,0:T(8,128)(2,1...) custom-call(f32[1024,512]{1,0:T(8,128)} %bitcast.18, ...), custom_call_target="tpu_custom_call" | custom-call | flops 4294967296 | bytes 12582912 | tf_op jit(solution)/shard_map/pallas_call | solution.py:692
  43.3 3.8 %shard_map.189 = (f32[1024,512]{1,0:T(8,128)}, bf16[1024,512]{1,0:T(8,128)(2,1)}, bf16[1024,512]{1,0:T(8,128)(2,1)}, bf16[1024,512]{1,0:T(8,128)(2,1)}, bf16[102...) custom-call(f32[1024,512]{1,0:T(8,128)S(1)} %get-tuple-element.26.refs_0_, ...), custom_call_target="tpu_custom_call" | custom-call | flops 209715200 | bytes 8388608 | tf_op jit(solution)/shard_map/pallas_call | solution.py:720
Async XLA Ops:
  0.6 1.2 %copy-start = (bf16[1,1024,512]{2,1,0:T(8,128)(2,1)S(1)}, bf16[1,1024,512]{2,1,0:T(8,128)(2,1)}, u32[]{:S(2)}) copy-start(bf16[1,1024,512]{2,1,0:T(8,128)(2,1)} %param.14) | copy-start | bytes 3145732
  1.9 0.7 %copy-start.1 = (s32[16,2,64]{2,1,0:T(2,128)S(1)}, s32[16,2,64]{2,1,0:T(2,128)}, u32[]{:S(2)}) copy-start(s32[16,2,64]{2,1,0:T(2,128)} %refs_12_.1) | copy-start | bytes 24580
  2.6 0.7 %copy-start.2 = (s32[1,1024]{1,0:T(1,128)S(1)}, s32[1,1024]{1,0:T(1,128)}, u32[]{:S(2)}) copy-start(s32[1,1024]{1,0:T(1,128)} %refs_8_.1) | copy-start | bytes 12292
where the time goes:
time: 47.4 us; the launch traced here: 47.2 us
  Pallas kernels  43.9 us (93%)
  local copies, waits for them, and re-layouts  2.62 us (6%)
  between operations  0.66 us (1%)
    pallas_call x1, Pallas kernels, fused_step(): pl.pallas_call(functools.partial(step_kernel, blk_count, chunks), out_sha...  40 us
    pallas_call x1, Pallas kernels, fused_step(): pl.pallas_call(functools.partial(finish_kernel, entries), out_shape=(jax....  3.84 us
    unnamed x6, local copies, waits for them, and re-layouts  2.62 us

commit v1 on v0

--- a/solution.py
+++ b/solution.py
@@ -281,6 +281,7 @@
 
 IMAGES = 6
 PACK = 16
+WIDE = 256
 QUERY_ROWS = 224
 KEY_ROWS = 256
 MESH = pl.DeviceIdType.MESH
@@ -291,6 +292,7 @@
     for count in range(3, IMAGES):
         need = -(-(count * SEG_MOST - local) // 16) * 16
         edges.append(min(local, max(need, edges[-1])))
+    edges.insert(-1, edges[-1] - 2 * PACK)
     edges.append(local)
     return list(zip(edges[:-1], edges[1:]))
 
@@ -329,6 +331,8 @@
     lane = lax.broadcasted_iota(jnp.int32, (1, pair), 1)
     first = jnp.where(lane < HD, 1.0, 0.0).astype(jnp.bfloat16)
     second = jnp.where(lane < HD, 0.0, 1.0).astype(jnp.bfloat16)
+    scale = jnp.bfloat16(HD ** (-0.5))
+    first_scaled, second_scaled = first * scale, second * scale
     query_block = window_start(low, qs, QUERY_ROWS)
     key_block = window_start(low, qs, KEY_ROWS)
     position = lax.broadcasted_iota(jnp.int32, (1, KEY_ROWS), 1) + key_block * PACK
@@ -336,7 +340,7 @@
     row = lax.broadcasted_iota(jnp.int32, (QUERY_ROWS, pair), 0) + query_block * PACK
     inside = (row >= low) & (row < high)
 
-    @pl.loop(0, width // pair, unroll=2)
+    @pl.loop(0, width // pair, unroll=4)
     def _(index):
         columns = pl.ds(pl.multiple_of(index * pair, pair), pair)
         query = window(qs, query_block, QUERY_ROWS, columns)
@@ -344,15 +348,13 @@
         keyed = window(ks, key_block, KEY_ROWS, columns)
         valued = window(vs, key_block, KEY_ROWS, columns)
         queries = jnp.concatenate([query * first, query * second], axis=0)
-        outers = jnp.concatenate([outer * first, outer * second], axis=0)
+        outers = jnp.concatenate([outer * first_scaled, outer * second_scaled], axis=0)
         scores = contract(queries, keyed, 1, 1) + bias
         out_proj = contract(outers, valued, 1, 1)
         exponent = jnp.exp(scores - jnp.max(scores, axis=-1, keepdims=True))
         inverse = 1.0 / jnp.sum(exponent, axis=-1, keepdims=True)
         centre = jnp.sum(exponent * out_proj, axis=-1, keepdims=True) * inverse
-        score_grad = (exponent * ((out_proj - centre) * (inverse * HD ** (-0.5)))).astype(
-            jnp.bfloat16
-        )
+        score_grad = (exponent * ((out_proj - centre) * inverse)).astype(jnp.bfloat16)
         both = jnp.dot(score_grad, keyed, preferred_element_type=jnp.float32)
         merged = jnp.where(lane < HD, both[:QUERY_ROWS], both[QUERY_ROWS:])
         qg[slot, :, columns] = jnp.where(inside, merged, 0.0).astype(jnp.bfloat16)
@@ -364,7 +366,8 @@
     (w_out, copy_out, mix_out, grad_out, new_out, held_out, tm, values, spread, total) = refs[13:23]
     (wt, cp, mx, tr, tc, gp, kw, vw, og, qw, upd, tok, recv) = refs[23:36]
     (qs, ks, vs, qg, acc, base, id_row, picks, heard, hot, part, slots, group, other) = refs[36:50]
-    (load_sem, send_tok, recv_tok, near, rise, fall, send_row, recv_row, sum_sem) = refs[50:]
+    selected, base_rows, copy_rows, grad_rows = refs[50:54]
+    (load_sem, send_tok, recv_tok, near, rise, fall, send_row, recv_row, sum_sem) = refs[54:]
 
     blk, tp = lax.axis_index("blk"), lax.axis_index("tp")
     planes = blk_count // 4
@@ -418,15 +421,14 @@
     ]
     for load in loads:
         load.start()
-    loads[0].wait()
     pl.semaphore_wait(barrier, 5 - lowest.astype(jnp.int32) - highest.astype(jnp.int32))
 
     sends = []
     for index, (start, end) in enumerate(chunks):
         size = end - start
-        first = blocks * tp + jnp.where(tp == 0, blocks - end, start)
+        first = jnp.where(tp == 0, blocks - end, start)
         send = pltpu.make_async_remote_copy(
-            tok.at[pl.ds(first, size)],
+            tokens.at[pl.ds(first, size)],
             recv.at[start:end],
             send_tok.at[index],
             recv_tok.at[index],
@@ -438,9 +440,9 @@
 
     pl.semaphore_signal(near.at[0], inc=1, device_id=flip_two, device_id_type=MESH)
 
-    for target in (qs, ks, vs, tok):
+    for target in (qs, ks, vs, tok, selected):
         target[far] = jnp.zeros((blocks,) + target.shape[1:], jnp.bfloat16)
-    for load in loads[1:7]:
+    for load in loads[:7]:
         load.wait()
 
     for stream, target in enumerate((hot, spread)):
@@ -490,6 +492,8 @@
         for target, weight in ((qs, qw), (ks, kw), (vs, vw)):
             result = jnp.dot(flat, weight[...], preferred_element_type=jnp.float32)
             target[rows] = result.astype(jnp.bfloat16).reshape(-1, PACK, width)
+        columns = contract(flat, spread[middle, :], 1, 1)
+        selected[rows] = columns.astype(jnp.bfloat16).reshape(-1, PACK, kept)
 
     loads[7].wait()
     loads[8].wait()
@@ -543,20 +547,44 @@
     take(0)
     attend_image(2, *bounds(2), qs, ks, vs, og, qg)
 
+    for load in loads[10:]:
+        load.wait()
+
+    @pl.loop(0, model_width // TILE)
+    def _(step):
+        rows = pl.ds(pl.multiple_of(step * TILE, TILE), TILE)
+        copy = tc[rows, :].astype(jnp.float32)
+        base[rows, :] = (
+            tr[rows, :].astype(jnp.float32)
+            + mixing_rate * (tm[rows, :].astype(jnp.float32) - copy)
+            - gp[rows, :].astype(jnp.float32)
+        )
+
+    def rows_of(source):
+        return jnp.dot(spread[middle, :], source[...], preferred_element_type=jnp.float32)
+
+    copy_rows[...] = rows_of(tc)
+    base_rows[...] = (
+        rows_of(tr) + mixing_rate * (rows_of(tm) - copy_rows[...]) - rows_of(gp)
+    )
+
+    take(1)
+    attend_image(3, *bounds(3), qs, ks, vs, og, qg)
+
     for move in param:
         move.wait()
     part[...] = jnp.zeros_like(part)
 
-    @pl.loop(0, model_width // TILE)
+    @pl.loop(0, model_width // WIDE)
     def _(step):
-        rows = pl.ds(pl.multiple_of(step * TILE, TILE), TILE)
+        rows = pl.ds(pl.multiple_of(step * WIDE, WIDE), WIDE)
         gain = contract(hot[:, rows], heard[...], 0, 0) / 3.0
         new = (mx[rows, :].astype(jnp.float32) + gain).astype(jnp.bfloat16)
         mix_out[rows, :] = new
         gap = new.astype(jnp.float32) - copy_out[rows, :].astype(jnp.float32)
         square = gap * gap
         folded = sum(square[:, at : at + 128] for at in range(0, width, 128))
-        part[...] += jnp.sum(folded.reshape(TILE // 8, 8, 128), axis=0)
+        part[...] += jnp.sum(folded.reshape(WIDE // 8, 8, 128), axis=0)
 
     slots[pl.ds(blk, 1)] = part[...][None]
 
@@ -574,33 +602,32 @@
     def _(distance):
         share(distance).start()
 
-    for load in loads[10:]:
-        load.wait()
-
-    @pl.loop(0, model_width // TILE)
-    def _(step):
-        rows = pl.ds(pl.multiple_of(step * TILE, TILE), TILE)
-        copy = tc[rows, :].astype(jnp.float32)
-        base[rows, :] = (
-            tr[rows, :].astype(jnp.float32)
-            + mixing_rate * (tm[rows, :].astype(jnp.float32) - copy)
-            - gp[rows, :].astype(jnp.float32)
-        )
-
-    take(1)
-    attend_image(3, *bounds(3), qs, ks, vs, og, qg)
-
-    def product(slots_used, rows):
+
+    def product(source, slots_used, columns):
         result = 0.0
         for slot in slots_used:
-            block = window_start(bounds(slot)[0], tok, QUERY_ROWS)
-            result += contract(window(tok, block, QUERY_ROWS, rows), qg[slot], 0, 0)
+            block = window_start(bounds(slot)[0], source, QUERY_ROWS)
+            result += contract(window(source, block, QUERY_ROWS, columns), qg[slot], 0, 0)
         return result
 
-    @pl.loop(0, model_width // TILE)
+    grad_rows[...] = product(selected, range(4), slice(None))
+
+    @pl.loop(0, model_width // WIDE)
     def _(step):
-        rows = pl.ds(pl.multiple_of(step * TILE, TILE), TILE)
-        acc[rows, :] = product(range(4), rows)
+        rows = pl.ds(pl.multiple_of(step * WIDE, WIDE), WIDE)
+        acc[rows, :] = product(tok, range(4), rows)
+
+    take(2)
+    take(3)
+    attend_image(4, *bounds(4), qs, ks, vs, og, qg)
+    take(4)
+    attend_image(5, *bounds(5), qs, ks, vs, og, qg)
+
+    gradient = grad_rows[...] + product(selected, (4, 5), slice(None))
+    grad = (gradient * model_width ** (-0.5)).astype(jnp.bfloat16)
+    new = (base_rows[...] + grad.astype(jnp.float32)).astype(jnp.bfloat16)
+    values[middle, :] = (new.astype(jnp.float32) - copy_rows[...]).astype(jnp.bfloat16)
+    track = swap(values, values, 1)
 
     most = pl.ds(0, blk_count - 1)
     for way in range(2):
@@ -611,30 +638,19 @@
     )
     cross.start()
 
-    take(2)
-    attend_image(4, *bounds(4), qs, ks, vs, og, qg)
-    take(3)
-    attend_image(5, *bounds(5), qs, ks, vs, og, qg)
-
-    @pl.loop(0, model_width // TILE)
+    @pl.loop(0, model_width // WIDE)
     def _(step):
-        start = pl.multiple_of(step * TILE, TILE)
-        rows = pl.ds(start, TILE)
-        gradient = acc[rows, :] + product((4, 5), rows)
+        start = pl.multiple_of(step * WIDE, WIDE)
+        rows = pl.ds(start, WIDE)
+        gradient = acc[rows, :] + product(tok, (4, 5), rows)
         grad = (gradient * model_width ** (-0.5)).astype(jnp.bfloat16)
         copy = tc[rows, :].astype(jnp.float32)
         new = (base[rows, :] + grad.astype(jnp.float32)).astype(jnp.bfloat16)
         change = new.astype(jnp.float32) - copy
-        picked = picked_mask(picks, blk, 1, start, TILE)
+        picked = picked_mask(picks, blk, 1, start, WIDE)
         grad_out[rows, :] = grad
         new_out[rows, :] = new
         held_out[rows, :] = jnp.where(picked > 0.5, copy + change, copy).astype(jnp.bfloat16)
-        upd[rows, :] = change.astype(jnp.bfloat16)
-
-    values[middle, :] = jnp.dot(
-        spread[middle, :], upd[...], preferred_element_type=jnp.float32
-    ).astype(jnp.bfloat16)
-    track = swap(values, values, 1)
 
     cross.wait()
     total[...] = group[...] + other[...]
@@ -702,6 +718,8 @@
         + [pltpu.VMEM((IMAGES, QUERY_ROWS, width), bf16), wide, wide]
         + [pltpu.VMEM(ids.shape, jnp.int32), pltpu.VMEM(row_picks.shape, jnp.int32), heard, hot]
         + [lanes, pltpu.VMEM((blk_count, 8, 128), f32), lanes, lanes]
+        + [pltpu.VMEM((total_rows // PACK, PACK, kept), bf16)]
+        + [pltpu.VMEM((kept, width), f32)] * 3
         + [dma((13,)), dma((len(chunks),)), dma((len(chunks),))]
         + [pltpu.SemaphoreType.REGULAR((2,))]
         + [pltpu.SemaphoreType.REGULAR((max(planes - 2, 1),))] * 2
@@ -714,7 +732,7 @@
             bytes_accessed=24 * model_width * width,
             transcendentals=total_rows * 256 * width // HD,
         ),
-    )(*arrays)
+    )(*(pltpu.with_memory_space_constraint(array, pltpu.HBM) for array in arrays))
     flat = jax.ShapeDtypeStruct((model_width, width), bf16)
     entries = float(blk_count * model_width * model_width)
     outs = pl.pallas_call(

time: 47.4 us -> 41.2 us (0.87)
  Pallas kernels: 43.9 us -> 40.2 us
  local copies, waits for them, and re-layouts: 2.62 us -> 0 us
    pallas_call x1, Pallas kernels: 40 us -> 36.4 us  [fused_step(): pl.pallas_call(functools.partial(step_kernel, blk_count, chunks), out_sha...]
    unnamed x6 -> x0, local copies, waits for them, and re-layouts: 2.62 us -> none
where the time goes in v1:
time: 41.2 us; the launch traced here: 41.1 us
  Pallas kernels  40.2 us (98%)
  between operations  0.81 us (2%)
    pallas_call x1, Pallas kernels, fused_step(): pl.pallas_call(functools.partial(step_kernel, blk_count, chunks), out_sha...  36.4 us
    pallas_call x1, Pallas kernels, fused_step(): pl.pallas_call(functools.partial(finish_kernel, entries), out_shape=(jax....  3.84 us

profile of v1, /device:TPU:0, one launch (start us, length us, event | category | flops | bytes accessed | tf_op | source)
XLA Modules:
  0.0 41.1 jit_solution(1284166234322101428)
XLA Ops:
  0.6 36.4 %shard_map.188 = (f32[1024,512]{1,0:T(8,128)S(1)}, bf16[1024,512]{1,0:T(8,128)(2,1)S(1)}, bf16[1024,512]{1,0:T(8,128)(2,1)S(1)}, bf16[1024,512]{1,0:T(8,128)(2,1...) custom-call(f32[1024,512]{1,0:T(8,128)} %bitcast.17, ...), custom_call_target="tpu_custom_call" | custom-call | flops 4294967296 | bytes 12582912 | tf_op jit(solution)/shard_map/pallas_call | solution.py:708
  37.0 3.8 %shard_map.189 = (f32[1024,512]{1,0:T(8,128)}, bf16[1024,512]{1,0:T(8,128)(2,1)}, bf16[1024,512]{1,0:T(8,128)(2,1)}, bf16[1024,512]{1,0:T(8,128)(2,1)}, bf16[102...) custom-call(f32[1024,512]{1,0:T(8,128)S(1)} %get-tuple-element.26.refs_0_, ...), custom_call_target="tpu_custom_call" | custom-call | flops 209715200 | bytes 8388608 | tf_op jit(solution)/shard_map/pallas_call | solution.py:738

commit v2 on v1

--- a/solution.py
+++ b/solution.py
@@ -325,7 +325,7 @@
     return jnp.concatenate(parts, axis=0)
 
 
-def attend_image(slot, low, high, qs, ks, vs, og, qg):
+def attend_image(slot, low, high, qs, ks, vs, og, qg, staged):
     width = qs.shape[2]
     pair = 2 * HD
     lane = lax.broadcasted_iota(jnp.int32, (1, pair), 1)
@@ -340,17 +340,22 @@
     row = lax.broadcasted_iota(jnp.int32, (QUERY_ROWS, pair), 0) + query_block * PACK
     inside = (row >= low) & (row < high)
 
-    @pl.loop(0, width // pair, unroll=4)
-    def _(index):
-        columns = pl.ds(pl.multiple_of(index * pair, pair), pair)
+    def start(index):
+        columns = pl.ds(index * pair, pair)
         query = window(qs, query_block, QUERY_ROWS, columns)
         outer = window(og, query_block, QUERY_ROWS, columns)
         keyed = window(ks, key_block, KEY_ROWS, columns)
         valued = window(vs, key_block, KEY_ROWS, columns)
         queries = jnp.concatenate([query * first, query * second], axis=0)
         outers = jnp.concatenate([outer * first_scaled, outer * second_scaled], axis=0)
-        scores = contract(queries, keyed, 1, 1) + bias
-        out_proj = contract(outers, valued, 1, 1)
+        staged[2 * (index % 2)] = contract(queries, keyed, 1, 1)
+        staged[2 * (index % 2) + 1] = contract(outers, valued, 1, 1)
+
+    def finish(index):
+        columns = pl.ds(index * pair, pair)
+        keyed = window(ks, key_block, KEY_ROWS, columns)
+        scores = staged[2 * (index % 2)] + bias
+        out_proj = staged[2 * (index % 2) + 1]
         exponent = jnp.exp(scores - jnp.max(scores, axis=-1, keepdims=True))
         inverse = 1.0 / jnp.sum(exponent, axis=-1, keepdims=True)
         centre = jnp.sum(exponent * out_proj, axis=-1, keepdims=True) * inverse
@@ -359,6 +364,13 @@
         merged = jnp.where(lane < HD, both[:QUERY_ROWS], both[QUERY_ROWS:])
         qg[slot, :, columns] = jnp.where(inside, merged, 0.0).astype(jnp.bfloat16)
 
+    pairs = width // pair
+    start(0)
+    for index in range(pairs):
+        if index + 1 < pairs:
+            start(index + 1)
+        finish(index)
+
 
 def step_kernel(blk_count, chunks, *refs):
     (weights, copies, mixed, tracker, tracker_copy, tracker_mixed, grad_prev) = refs[:7]
@@ -366,8 +378,8 @@
     (w_out, copy_out, mix_out, grad_out, new_out, held_out, tm, values, spread, total) = refs[13:23]
     (wt, cp, mx, tr, tc, gp, kw, vw, og, qw, upd, tok, recv) = refs[23:36]
     (qs, ks, vs, qg, acc, base, id_row, picks, heard, hot, part, slots, group, other) = refs[36:50]
-    selected, base_rows, copy_rows, grad_rows = refs[50:54]
-    (load_sem, send_tok, recv_tok, near, rise, fall, send_row, recv_row, sum_sem) = refs[54:]
+    selected, base_rows, copy_rows, grad_rows, staged = refs[50:55]
+    (load_sem, send_tok, recv_tok, near, rise, fall, send_row, recv_row, sum_sem) = refs[55:]
 
     blk, tp = lax.axis_index("blk"), lax.axis_index("tp")
     planes = blk_count // 4
@@ -508,14 +520,14 @@
         tell(fall.at[stage], rise.at[stage])
         if stage == 0:
             loads[9].wait()
-            attend_image(0, *bounds(0), qs, ks, vs, og, qg)
+            attend_image(0, *bounds(0), qs, ks, vs, og, qg, staged)
         if stage == 1:
-            attend_image(1, *bounds(1), qs, ks, vs, og, qg)
+            attend_image(1, *bounds(1), qs, ks, vs, og, qg, staged)
         hear(fall.at[stage], rise.at[stage])
     if planes < 3:
         loads[9].wait()
     for slot in range(min(2, planes - 2), 2):
-        attend_image(slot, *bounds(slot), qs, ks, vs, og, qg)
+        attend_image(slot, *bounds(slot), qs, ks, vs, og, qg, staged)
 
     def swap(source, target, index):
         moves = []
@@ -545,7 +557,7 @@
         project_block(block, rows)
 
     take(0)
-    attend_image(2, *bounds(2), qs, ks, vs, og, qg)
+    attend_image(2, *bounds(2), qs, ks, vs, og, qg, staged)
 
     for load in loads[10:]:
         load.wait()
@@ -567,9 +579,6 @@
     base_rows[...] = (
         rows_of(tr) + mixing_rate * (rows_of(tm) - copy_rows[...]) - rows_of(gp)
     )
-
-    take(1)
-    attend_image(3, *bounds(3), qs, ks, vs, og, qg)
 
     for move in param:
         move.wait()
@@ -603,6 +612,9 @@
         share(distance).start()
 
 
+    take(1)
+    attend_image(3, *bounds(3), qs, ks, vs, og, qg, staged)
+
     def product(source, slots_used, columns):
         result = 0.0
         for slot in slots_used:
@@ -619,9 +631,9 @@
 
     take(2)
     take(3)
-    attend_image(4, *bounds(4), qs, ks, vs, og, qg)
+    attend_image(4, *bounds(4), qs, ks, vs, og, qg, staged)
     take(4)
-    attend_image(5, *bounds(5), qs, ks, vs, og, qg)
+    attend_image(5, *bounds(5), qs, ks, vs, og, qg, staged)
 
     gradient = grad_rows[...] + product(selected, (4, 5), slice(None))
     grad = (gradient * model_width ** (-0.5)).astype(jnp.bfloat16)
@@ -720,6 +732,7 @@
         + [lanes, pltpu.VMEM((blk_count, 8, 128), f32), lanes, lanes]
         + [pltpu.VMEM((total_rows // PACK, PACK, kept), bf16)]
         + [pltpu.VMEM((kept, width), f32)] * 3
+        + [pltpu.VMEM((4, 2 * QUERY_ROWS, KEY_ROWS), f32)]
         + [dma((13,)), dma((len(chunks),)), dma((len(chunks),))]
         + [pltpu.SemaphoreType.REGULAR((2,))]
         + [pltpu.SemaphoreType.REGULAR((max(planes - 2, 1),))] * 2

time: 41.2 us -> 40.4 us (0.981)
  Pallas kernels: 40.2 us -> 39.4 us
    pallas_call x1, Pallas kernels: 36.4 us -> 35.6 us  [fused_step(): pl.pallas_call(functools.partial(step_kernel, blk_count, chunks), out_sha...]
where the time goes in v2:
time: 40.4 us; the launch traced here: 40.2 us
  Pallas kernels  39.4 us (98%)
  between operations  0.81 us (2%)
    pallas_call x1, Pallas kernels, fused_step(): pl.pallas_call(functools.partial(step_kernel, blk_count, chunks), out_sha...  35.6 us
    pallas_call x1, Pallas kernels, fused_step(): pl.pallas_call(functools.partial(finish_kernel, entries), out_shape=(jax....  3.84 us

profile of v2, /device:TPU:0, one launch (start us, length us, event | category | flops | bytes accessed | tf_op | source)
XLA Modules:
  0.0 40.2 jit_solution(9321199630467821756)
XLA Ops:
  0.6 35.6 %shard_map.188 = (f32[1024,512]{1,0:T(8,128)S(1)}, bf16[1024,512]{1,0:T(8,128)(2,1)S(1)}, bf16[1024,512]{1,0:T(8,128)(2,1)S(1)}, bf16[1024,512]{1,0:T(8,128)(2,1...) custom-call(f32[1024,512]{1,0:T(8,128)} %bitcast.17, ...), custom_call_target="tpu_custom_call" | custom-call | flops 4294967296 | bytes 12582912 | tf_op jit(solution)/shard_map/pallas_call | solution.py:720
  36.2 3.8 %shard_map.189 = (f32[1024,512]{1,0:T(8,128)}, bf16[1024,512]{1,0:T(8,128)(2,1)}, bf16[1024,512]{1,0:T(8,128)(2,1)}, bf16[1024,512]{1,0:T(8,128)(2,1)}, bf16[102...) custom-call(f32[1024,512]{1,0:T(8,128)S(1)} %get-tuple-element.26.refs_0_, ...), custom_call_target="tpu_custom_call" | custom-call | flops 209715200 | bytes 8388608 | tf_op jit(solution)/shard_map/pallas_call | solution.py:751
